TPU v7x, 32 devices: a whole 2x2x4 slice. The times are simulated.
32 devices in a mesh: row: 8 (over z, y), col: 4 (over x, core).
Axes of the slice: x: 2, y: 2, z: 4, core: 2. Of those that a mesh axis runs over, the one named last changes fastest.
Arguments:
- prior: float32 [2, 4096, 4096], P(None, 'row', 'col'), may hold values from 0.1 to 10
- first_tiles: bfloat16 [2, 32, 24, 128, 128], P(None, 'row'), may hold values from 0 to 1
- first_columns: int32 [2, 32, 24], P(None, 'row'), may hold values from 0 to 31, as said below
- first_counts: int32 [2, 32], P(None, 'row'), may hold values from 1 to 24, as said below
- second_network_tiles: bfloat16 [2, 32, 24, 128, 128], P(None, 'col'), may hold values from 0 to 1
- second_columns: int32 [2, 32, 24], P(None, 'col'), may hold values from 0 to 31, as said below
- second_counts: int32 [2, 32], P(None, 'col'), may hold values from 1 to 24, as said below
- sizes_first: int32 [2], replicated, may hold values from 2048 to 4096
- sizes_second: int32 [2], replicated, may hold values from 2048 to 4096
Outputs:
- similarity: float32 [2, 4096, 4096], P(None, 'row', 'col')
Inputs may be any that keep to these rules, and one draw needn't show every extreme that they name: `first_columns`: within a tile row the 24 slots name distinct tile columns. Only the first first_counts[p, i] slots of tile row i are live; in every pair some tile row has all 24 live. `second_columns`: within a tile row the 24 slots name distinct tile columns. Only the first second_counts[p, i] slots of tile row i are live; in every pair some tile row has all 24 live.
All inputs are finite; a program needn't handle non-finite values.
Results may differ from a plain program's by a relative error of at most 0.00035.
Values may be sent and summed in bfloat16 or wider, within the bound.
A program may use at most 128 MiB of HBM per device.

v0:
```python
import jax
import jax.numpy as jnp
from jax import lax
from jax.sharding import PartitionSpec as P

ITERS = 2
propagation = 0.7


def first_local(tiles, columns, counts, panel):
    local_rows = tiles.shape[0]
    tile_size = tiles.shape[2]
    width = panel.shape[1]
    blocks = panel.reshape(-1, tile_size, width)
    selected_entries = blocks[columns]
    in_use = jnp.arange(tiles.shape[1])[None, :] < counts[:, None]
    masked_entries = jnp.where(in_use[:, :, None, None], tiles, jnp.zeros((), tiles.dtype))
    similarity_output = jnp.einsum(
        "hgfu,hguq->hfq", masked_entries, selected_entries, preferred_element_type=jnp.float32
    )
    return similarity_output.reshape(local_rows * tile_size, width)


def second_local(tiles, columns, counts, gathered):
    local_rows = tiles.shape[0]
    tile_size = tiles.shape[2]
    height = gathered.shape[0]
    blocks = gathered.reshape(height, -1, tile_size)
    selected_entries = blocks[:, columns]
    in_use = jnp.arange(tiles.shape[1])[None, :] < counts[:, None]
    masked_entries = jnp.where(in_use[:, :, None, None], tiles, jnp.zeros((), tiles.dtype))
    similarity_output = jnp.einsum(
        "rtsk,tsck->rtc", selected_entries, masked_entries, preferred_element_type=jnp.float32
    )
    return similarity_output.reshape(height, local_rows * tile_size)


def advance(
    current,
    initial,
    active,
    entries,
    first_network_tiles,
    f_columns,
    f_counts,
    s_tiles,
    s_columns,
    s_counts,
):
    resident_panel_block = current.astype(jnp.bfloat16)
    panel = lax.all_gather(resident_panel_block, "row", axis=1, tiled=True)
    product = jnp.stack([first_local(first_network_tiles[0], f_columns[0], f_counts[0], panel[0])])
    product = product.astype(jnp.bfloat16)
    gathered = lax.all_gather(product, "col", axis=2, tiled=True)
    image = jnp.stack([second_local(s_tiles[0], s_columns[0], s_counts[0], gathered[0])])
    image = jnp.where(active, image, jnp.float32(0.0))
    square_sum = lax.psum(jnp.sum(image * image, axis=(1, 2)), ("row", "col"))
    divisor = jnp.sqrt(square_sum / entries + 1e-06)
    return propagation * image / divisor[:, None, None] + (1.0 - propagation) * initial


def shards(
    prior,
    first_tiles,
    first_columns,
    first_counts,
    second_network_tiles,
    second_columns,
    second_counts,
    sizes_first,
    sizes_second,
):
    pair_count, row_count, col_count = prior.shape
    row_index = lax.axis_index("row") * row_count + jnp.arange(row_count, dtype=jnp.int32)
    col_index = lax.axis_index("col") * col_count + jnp.arange(col_count, dtype=jnp.int32)
    active = (row_index[None, :, None] < sizes_first[:, None, None]) & (
        col_index[None, None, :] < sizes_second[:, None, None]
    )
    initial = jnp.where(active, prior, jnp.float32(0.0))
    entries = sizes_first.astype(jnp.float32) * sizes_second.astype(jnp.float32)
    current = initial
    for iteration in range(ITERS):
        updated = []
        for pair_index in range(pair_count):
            upper = pair_index + 1
            updated.append(
                advance(
                    current[pair_index:upper],
                    initial[pair_index:upper],
                    active[pair_index:upper],
                    entries[pair_index:upper],
                    first_tiles[pair_index:upper],
                    first_columns[pair_index:upper],
                    first_counts[pair_index:upper],
                    second_network_tiles[pair_index:upper],
                    second_columns[pair_index:upper],
                    second_counts[pair_index:upper],
                )
            )
        current = jnp.concatenate(updated, axis=0)
    return current


def solution(mesh):
    in_specs = (
        P(None, "row", "col"),
        P(None, "row", None, None, None),
        P(None, "row", None),
        P(None, "row"),
        P(None, "col", None, None, None),
        P(None, "col", None),
        P(None, "col"),
        P(),
        P(),
    )
    out_specs = P(None, "row", "col")
    return jax.shard_map(shards, mesh=mesh, in_specs=in_specs, out_specs=out_specs, check_vma=False)
```

profile of v0, /device:TPU:0, one launch (start us, length us, event | category | flops | bytes accessed | tf_op | source)
XLA Modules:
  0.0 844.6 jit_solution(2062341585849978496)
XLA Ops:
  15.4 126.4 %all-gather.17.cloned.1.call-done = bf16[1,4096,1024]{2,1,0:T(8,128)(2,1)} async-done(((bf16[1,512,1024]{2,1,0:T(8,128)(2,1)}), bf16[1,4096,1024]{2,1,0:T(8,128)(2,1)}) %all-gather.17.cloned.1.call-update) | async-done | bytes 8388624 | tf_op jit(solution)/shard_map/all_gather | solution.py:51
  141.8 14.0 %gather_fusion.4 = bf16[96,128,1024]{2,1,0:T(8,128)(2,1)} fusion(bf16[32,128,1024]{2,1,0:T(8,128)(2,1)} %bitcast.129, s32[1024]{0:T(1024)S(1)} %pad_clamp_fusion.1), kind=kCustom, calls=%fused_computation.4 | custom fusion | bytes 50332032 | tf_op jit(solution)/shard_map/gather | solution.py:15
  155.8 11.1 %bitcast_convert_fusion.1 = bf16[4,128,1024]{2,1,0:T(8,128)(2,1)S(1)} fusion(bf16[4,24,128,1024]{3,2,1,0:T(8,128)(2,1)} %bitcast.138, bf16[2,4,24,128,128]{4,3,2,1,0:T(8,128)(2,1)} %param.10, pred[4,24]{1,0:T(4,128)(4,1)S(1)} %get-tuple-element.29), kind=kOutput, calls=%fused_computation.26 | convolution fusion | flops 3223322624 | bytes 29360224 | tf_op jit(solution)/shard_map/hgfu,hguq->hfq/dot_general | solution.py:18
  168.4 98.2 %all-gather.9.cloned.1.call-done = bf16[1,4096,1024]{2,1,0:T(8,128)(2,1)} async-done(((bf16[1,512,1024]{2,1,0:T(8,128)(2,1)}), bf16[1,4096,1024]{2,1,0:T(8,128)(2,1)}) %all-gather.9.cloned.1.call-update) | async-done | bytes 8388624 | tf_op jit(solution)/shard_map/all_gather | solution.py:51
  266.6 14.3 %gather_fusion = bf16[96,128,1024]{2,1,0:T(8,128)(2,1)} fusion(bf16[32,128,1024]{2,1,0:T(8,128)(2,1)} %bitcast.128, s32[1024]{0:T(1024)S(1)} %pad_clamp_fusion.3), kind=kCustom, calls=%fused_computation | custom fusion | bytes 50332032 | tf_op jit(solution)/shard_map/gather | solution.py:15
  280.9 11.2 %bitcast_convert_fusion.3 = bf16[4,128,1024]{2,1,0:T(8,128)(2,1)S(1)} fusion(bf16[4,24,128,1024]{3,2,1,0:T(8,128)(2,1)} %bitcast.136, bf16[2,4,24,128,128]{4,3,2,1,0:T(8,128)(2,1)} %param.10, pred[4,24]{1,0:T(4,128)(4,1)S(1)} %get-tuple-element.30), kind=kOutput, calls=%fused_computation.28 | convolution fusion | flops 3223322624 | bytes 29360224 | tf_op jit(solution)/shard_map/hgfu,hguq->hfq/dot_general | solution.py:18
  307.2 13.7 %gather_fusion.5 = bf16[192,512,128]{2,1,0:T(8,128)(2,1)} fusion(bf16[512,32,128]{2,0,1:T(8,128)(2,1)} %copy.25, s32[1024]{0:T(1024)S(1)} %pad_clamp_fusion), kind=kCustom, calls=%fused_computation.5 | custom fusion | bytes 50332416 | tf_op jit(solution)/shard_map/gather | solution.py:29
  321.0 15.3 %fusion.3 = f32[8,128,512,1]{2,1,3,0:T(8,128)} fusion(bf16[512,8,24,128]{3,0,2,1:T(8,128)(2,1)} %bitcast.139, bf16[2,8,24,128,128]{4,3,2,1,0:T(8,128)(2,1)} %param.13, pred[8,24]{1,0:T(8,128)(4,1)S(1)} %get-tuple-element.31), kind=kOutput, calls=%fused_computation.13 | convolution fusion | flops 3224371200 | bytes 33554624 | tf_op jit(solution)/shard_map/rtsk,tsck->rtc/dot_general | solution.py:32
  338.2 6.4 copy.19
  344.7 13.4 %gather_fusion.1 = bf16[192,512,128]{2,1,0:T(8,128)(2,1)} fusion(bf16[512,32,128]{2,0,1:T(8,128)(2,1)} %copy.19, s32[1024]{0:T(1024)S(1)} %pad_clamp_fusion.2), kind=kCustom, calls=%fused_computation.1 | custom fusion | bytes 50332416 | tf_op jit(solution)/shard_map/gather | solution.py:29
  358.0 15.2 %fusion.1 = f32[8,128,512,1]{2,1,3,0:T(8,128)} fusion(bf16[512,8,24,128]{3,0,2,1:T(8,128)(2,1)} %bitcast.137, bf16[2,8,24,128,128]{4,3,2,1,0:T(8,128)(2,1)} %param.13, pred[8,24]{1,0:T(8,128)(4,1)S(1)} %get-tuple-element.32), kind=kOutput, calls=%fused_computation.11 | convolution fusion | flops 3224371200 | bytes 33554624 | tf_op jit(solution)/shard_map/rtsk,tsck->rtc/dot_general | solution.py:32
  379.0 39.4 %all-reduce.1 = (f32[1]{0:T(128)}, f32[1]{0:T(128)}) all-reduce(f32[1]{0:T(128)} %bitcast.52, f32[1]{0:T(128)} %bitcast.18), channel_id=1, replica_groups=mesh['row'=8,'col'=4] {'row','col'}, use_global_device_ids=true, to_apply=%region_5.6 | all-reduce | flops 2 | bytes 16 | tf_op jit(solution)/shard_map/psum | solution.py:57
  427.1 125.0 %all-gather.21.cloned.1.call-done = bf16[1,4096,1024]{2,1,0:T(8,128)(2,1)} async-done(((bf16[1,512,1024]{2,1,0:T(8,128)(2,1)}), bf16[1,4096,1024]{2,1,0:T(8,128)(2,1)}) %all-gather.21.cloned.1.call-update) | async-done | bytes 8388624 | tf_op jit(solution)/shard_map/all_gather | solution.py:51
  552.2 14.1 %gather_fusion.6 = bf16[96,128,1024]{2,1,0:T(8,128)(2,1)} fusion(bf16[32,128,1024]{2,1,0:T(8,128)(2,1)} %bitcast.131, s32[1024]{0:T(1024)S(1)} %pad_clamp_fusion.1), kind=kCustom, calls=%fused_computation.6 | custom fusion | bytes 50332032 | tf_op jit(solution)/shard_map/gather | solution.py:15
  566.3 11.1 %bitcast_convert_fusion = bf16[4,128,1024]{2,1,0:T(8,128)(2,1)S(1)} fusion(bf16[4,24,128,1024]{3,2,1,0:T(8,128)(2,1)} %bitcast.132, bf16[2,4,24,128,128]{4,3,2,1,0:T(8,128)(2,1)} %param.10, pred[4,24]{1,0:T(4,128)(4,1)S(1)} %get-tuple-element.29), kind=kOutput, calls=%fused_computation.25 | convolution fusion | flops 3223322624 | bytes 29360224 | tf_op jit(solution)/shard_map/hgfu,hguq->hfq/dot_general | solution.py:18
  579.0 97.8 %all-gather.13.cloned.1.call-done = bf16[1,4096,1024]{2,1,0:T(8,128)(2,1)} async-done(((bf16[1,512,1024]{2,1,0:T(8,128)(2,1)}), bf16[1,4096,1024]{2,1,0:T(8,128)(2,1)}) %all-gather.13.cloned.1.call-update) | async-done | bytes 8388624 | tf_op jit(solution)/shard_map/all_gather | solution.py:51
  676.9 14.3 %gather_fusion.2 = bf16[96,128,1024]{2,1,0:T(8,128)(2,1)} fusion(bf16[32,128,1024]{2,1,0:T(8,128)(2,1)} %bitcast.130, s32[1024]{0:T(1024)S(1)} %pad_clamp_fusion.3), kind=kCustom, calls=%fused_computation.2 | custom fusion | bytes 50332032 | tf_op jit(solution)/shard_map/gather | solution.py:15
  691.1 11.1 %bitcast_convert_fusion.2 = bf16[4,128,1024]{2,1,0:T(8,128)(2,1)S(1)} fusion(bf16[4,24,128,1024]{3,2,1,0:T(8,128)(2,1)} %bitcast.133, bf16[2,4,24,128,128]{4,3,2,1,0:T(8,128)(2,1)} %param.10, pred[4,24]{1,0:T(4,128)(4,1)S(1)} %get-tuple-element.30), kind=kOutput, calls=%fused_computation.27 | convolution fusion | flops 3223322624 | bytes 29360224 | tf_op jit(solution)/shard_map/hgfu,hguq->hfq/dot_general | solution.py:18
  703.6 7.5 all-gather.23.cloned.1.call-done
  717.5 13.7 %gather_fusion.7 = bf16[192,512,128]{2,1,0:T(8,128)(2,1)} fusion(bf16[512,32,128]{2,0,1:T(8,128)(2,1)} %copy.28, s32[1024]{0:T(1024)S(1)} %pad_clamp_fusion), kind=kCustom, calls=%fused_computation.7 | custom fusion | bytes 50332416 | tf_op jit(solution)/shard_map/gather | solution.py:29
  731.2 15.3 %fusion.2 = f32[8,128,512,1]{2,1,3,0:T(8,128)} fusion(bf16[512,8,24,128]{3,0,2,1:T(8,128)(2,1)} %bitcast.134, bf16[2,8,24,128,128]{4,3,2,1,0:T(8,128)(2,1)} %param.13, pred[8,24]{1,0:T(8,128)(4,1)S(1)} %get-tuple-element.31), kind=kOutput, calls=%fused_computation.12 | convolution fusion | flops 3224371200 | bytes 33554624 | tf_op jit(solution)/shard_map/rtsk,tsck->rtc/dot_general | solution.py:32
  755.0 13.4 %gather_fusion.3 = bf16[192,512,128]{2,1,0:T(8,128)(2,1)} fusion(bf16[512,32,128]{2,0,1:T(8,128)(2,1)} %copy.22, s32[1024]{0:T(1024)S(1)} %pad_clamp_fusion.2), kind=kCustom, calls=%fused_computation.3 | custom fusion | bytes 50332416 | tf_op jit(solution)/shard_map/gather | solution.py:29
  768.3 15.2 %fusion = f32[8,128,512,1]{2,1,3,0:T(8,128)} fusion(bf16[512,8,24,128]{3,0,2,1:T(8,128)(2,1)} %bitcast.135, bf16[2,8,24,128,128]{4,3,2,1,0:T(8,128)(2,1)} %param.13, pred[8,24]{1,0:T(8,128)(4,1)S(1)} %get-tuple-element.32), kind=kOutput, calls=%fused_computation.10 | convolution fusion | flops 3224371200 | bytes 33554624 | tf_op jit(solution)/shard_map/rtsk,tsck->rtc/dot_general | solution.py:32
  789.3 39.4 %all-reduce = (f32[1]{0:T(128)}, f32[1]{0:T(128)}) all-reduce(f32[1]{0:T(128)} %bitcast.66, f32[1]{0:T(128)} %bitcast.32), channel_id=1, replica_groups=mesh['row'=8,'col'=4] {'row','col'}, use_global_device_ids=true, to_apply=%region_7.8 | all-reduce | flops 2 | bytes 16 | tf_op jit(solution)/shard_map/psum | solution.py:57
  (72 shorter events, 69.2 us)
Async XLA Ops:
  6.5 135.2 %all-gather.17.cloned.1.call-start = ((), (), s32[]{:S(2)}) async-start(), calls=%async_computation.4 | async-start | bytes 9437184 | tf_op jit(solution)/shard_map/all_gather | solution.py:51
  10.7 2.0 copy-start
  12.7 2.5 copy-start.2
  12.7 2.6 copy-start.3
  14.4 252.2 %all-gather.9.cloned.1.call-start = ((), (), s32[]{:S(2)}) async-start(), calls=%async_computation | async-start | bytes 9437184 | tf_op jit(solution)/shard_map/all_gather | solution.py:51
  15.2 285.6 %all-gather.19.cloned.1.call-start = ((), (), s32[]{:S(2)}) async-start(), calls=%async_computation.5 | async-start | bytes 5242880 | tf_op jit(solution)/shard_map/all_gather | solution.py:54
  168.3 170.0 %all-gather.11.cloned.1.call-start = ((), (), s32[]{:S(2)}) async-start(), calls=%async_computation.1 | async-start | bytes 5242880 | tf_op jit(solution)/shard_map/all_gather | solution.py:54
  280.8 12.8 %copy-start.1 = (s32[2,8,24]{2,1,0:T(8,128)S(1)}, s32[2,8,24]{2,1,0:T(8,128)}, u32[]{:S(2)}) copy-start(s32[2,8,24]{2,1,0:T(8,128)} %param.14) | copy-start | bytes 4612
  280.9 13.0 %copy-start.5 = (s32[2]{0:T(128)S(1)}, s32[2]{0:T(128)}, u32[]{:S(2)}) copy-start(s32[2]{0:T(128)} %param.17) | copy-start | bytes 28
  280.9 13.0 %copy-start.6 = (s32[2]{0:T(128)S(1)}, s32[2]{0:T(128)}, u32[]{:S(2)}) copy-start(s32[2]{0:T(128)} %param.16) | copy-start | bytes 28
  280.9 13.6 %copy-start.4 = (s32[2,8]{1,0:T(2,128)S(1)}, s32[2,8]{1,0:T(2,128)}, u32[]{:S(2)}) copy-start(s32[2,8]{1,0:T(2,128)} %param.15) | copy-start | bytes 196
  293.4 258.8 %all-gather.21.cloned.1.call-start = ((), (), s32[]{:S(2)}) async-start(), calls=%async_computation.6 | async-start | bytes 9437184 | tf_op jit(solution)/shard_map/all_gather | solution.py:51
  426.5 250.3 %all-gather.13.cloned.1.call-start = ((), (), s32[]{:S(2)}) async-start(), calls=%async_computation.2 | async-start | bytes 9437184 | tf_op jit(solution)/shard_map/all_gather | solution.py:51
  427.1 284.0 %all-gather.23.cloned.1.call-start = ((), (), s32[]{:S(2)}) async-start(), calls=%async_computation.7 | async-start | bytes 5242880 | tf_op jit(solution)/shard_map/all_gather | solution.py:54
  578.7 169.8 %all-gather.15.cloned.1.call-start = ((), (), s32[]{:S(2)}) async-start(), calls=%async_computation.3 | async-start | bytes 5242880 | tf_op jit(solution)/shard_map/all_gather | solution.py:54
Sparse Core Ops, SparseCore 0:
  14.5 127.1 all-gather.16
  143.9 122.6 all-gather.8
  268.1 32.6 all-gather.18
  302.2 34.4 all-gather.10
  426.6 125.5 all-gather.20
  554.2 122.6 all-gather.12
  678.4 32.6 all-gather.22
  712.6 34.4 all-gather.14
where the time goes:
time: 846 us; the launch traced here: 845 us
  waiting for transfers between devices  462 us (55%)
  local copies, waits for them, and re-layouts  156 us (18%)
  matrix products  105 us (12%)
  blocking collectives  78.8 us (9%)
  other arithmetic  22.5 us (3%)
  between operations  19 us (2%)
    all_gather x4, waiting for transfers between devices, advance(): panel = lax.all_gather(resident_panel_block, 'row', axis=1, tiled=True)  447 us
    psum x2, blocking collectives, advance(): square_sum = lax.psum(jnp.sum(image * image, axis=(1, 2)), ('row', 'col'))  78.8 us
    dot_general x4, matrix products, second_local(): jnp.einsum('rtsk,tsck->rtc', selected_entries, masked_entries, preferred_...  61 us
    gather x4, local copies, waits for them, and re-layouts, first_local(): selected_entries = blocks[columns]  56.7 us
    gather x4, local copies, waits for them, and re-layouts, second_local(): selected_entries = blocks[:, columns]  54.2 us
    dot_general x4, matrix products, first_local(): jnp.einsum('hgfu,hguq->hfq', masked_entries, selected_entries, preferred_...  44.4 us
    another operation x4, local copies, waits for them, and re-layouts, second_local(): blocks = gathered.reshape(height, -1, tile_size)  25.8 us
  transfers between devices with their start and end apart: 8, of which 6 were waited for; matrix products, arithmetic and copies ran while one was open for 22% of the time, Pallas kernels for 0%

commit v1 on v0

--- a/solution.py
+++ b/solution.py
@@ -48,7 +48,7 @@
     s_counts,
 ):
     resident_panel_block = current.astype(jnp.bfloat16)
-    panel = lax.all_gather(resident_panel_block, "row", axis=1, tiled=True)
+    panel = jnp.concatenate(lax.all_gather(resident_panel_block, "row"), axis=1)
     product = jnp.stack([first_local(first_network_tiles[0], f_columns[0], f_counts[0], panel[0])])
     product = product.astype(jnp.bfloat16)
     gathered = lax.all_gather(product, "col", axis=2, tiled=True)

time: 846 us -> 846 us (level)
  no operation moved by 1% of the time
where the time goes in v1:
time: 846 us; the launch traced here: 845 us
  waiting for transfers between devices  462 us (55%)
  local copies, waits for them, and re-layouts  156 us (18%)
  matrix products  105 us (12%)
  blocking collectives  78.8 us (9%)
  other arithmetic  22.5 us (3%)
  between operations  19 us (2%)
    all_gather x4, waiting for transfers between devices, advance(): panel = jnp.concatenate(lax.all_gather(resident_panel_block, 'row'), axis=1)  447 us
    psum x2, blocking collectives, advance(): square_sum = lax.psum(jnp.sum(image * image, axis=(1, 2)), ('row', 'col'))  78.8 us
    dot_general x4, matrix products, second_local(): jnp.einsum('rtsk,tsck->rtc', selected_entries, masked_entries, preferred_...  61 us
    gather x4, local copies, waits for them, and re-layouts, first_local(): selected_entries = blocks[columns]  56.7 us
    gather x4, local copies, waits for them, and re-layouts, second_local(): selected_entries = blocks[:, columns]  54.2 us
    dot_general x4, matrix products, first_local(): jnp.einsum('hgfu,hguq->hfq', masked_entries, selected_entries, preferred_...  44.4 us
    another operation x4, local copies, waits for them, and re-layouts, second_local(): blocks = gathered.reshape(height, -1, tile_size)  25.8 us
  transfers between devices with their start and end apart: 8, of which 6 were waited for; matrix products, arithmetic and copies ran while one was open for 22% of the time, Pallas kernels for 0%

profile of v1, /device:TPU:0, one launch (start us, length us, event | category | flops | bytes accessed | tf_op | source)
XLA Modules:
  0.0 844.6 jit_solution(2062341585849978496)
XLA Ops:
  15.4 126.4 %all-gather.25.cloned.1.call-done = bf16[8,512,1024]{2,1,0:T(8,128)(2,1)} async-done(((bf16[1,512,1024]{2,1,0:T(8,128)(2,1)}), bf16[8,512,1024]{2,1,0:T(8,128)(2,1)}) %all-gather.25.cloned.1.call-update) | async-done | bytes 8388624 | tf_op jit(solution)/shard_map/all_gather | solution.py:51
  141.8 14.0 %gather_fusion.4 = bf16[96,128,1024]{2,1,0:T(8,128)(2,1)} fusion(bf16[32,128,1024]{2,1,0:T(8,128)(2,1)} %bitcast.129, s32[1024]{0:T(1024)S(1)} %pad_clamp_fusion.1), kind=kCustom, calls=%fused_computation.4 | custom fusion | bytes 50332032 | tf_op jit(solution)/shard_map/gather | solution.py:15
  155.8 11.1 %bitcast_convert_fusion.1 = bf16[4,128,1024]{2,1,0:T(8,128)(2,1)S(1)} fusion(bf16[4,24,128,1024]{3,2,1,0:T(8,128)(2,1)} %bitcast.138, bf16[2,4,24,128,128]{4,3,2,1,0:T(8,128)(2,1)} %param.10, pred[4,24]{1,0:T(4,128)(4,1)S(1)} %get-tuple-element.29), kind=kOutput, calls=%fused_computation.26 | convolution fusion | flops 3223322624 | bytes 29360224 | tf_op jit(solution)/shard_map/hgfu,hguq->hfq/dot_general | solution.py:18
  168.4 98.2 %all-gather.21.cloned.1.call-done = bf16[8,512,1024]{2,1,0:T(8,128)(2,1)} async-done(((bf16[1,512,1024]{2,1,0:T(8,128)(2,1)}), bf16[8,512,1024]{2,1,0:T(8,128)(2,1)}) %all-gather.21.cloned.1.call-update) | async-done | bytes 8388624 | tf_op jit(solution)/shard_map/all_gather | solution.py:51
  266.6 14.3 %gather_fusion = bf16[96,128,1024]{2,1,0:T(8,128)(2,1)} fusion(bf16[32,128,1024]{2,1,0:T(8,128)(2,1)} %bitcast.128, s32[1024]{0:T(1024)S(1)} %pad_clamp_fusion.3), kind=kCustom, calls=%fused_computation | custom fusion | bytes 50332032 | tf_op jit(solution)/shard_map/gather | solution.py:15
  280.9 11.2 %bitcast_convert_fusion.3 = bf16[4,128,1024]{2,1,0:T(8,128)(2,1)S(1)} fusion(bf16[4,24,128,1024]{3,2,1,0:T(8,128)(2,1)} %bitcast.136, bf16[2,4,24,128,128]{4,3,2,1,0:T(8,128)(2,1)} %param.10, pred[4,24]{1,0:T(4,128)(4,1)S(1)} %get-tuple-element.30), kind=kOutput, calls=%fused_computation.28 | convolution fusion | flops 3223322624 | bytes 29360224 | tf_op jit(solution)/shard_map/hgfu,hguq->hfq/dot_general | solution.py:18
  307.2 13.7 %gather_fusion.5 = bf16[192,512,128]{2,1,0:T(8,128)(2,1)} fusion(bf16[512,32,128]{2,0,1:T(8,128)(2,1)} %copy.37, s32[1024]{0:T(1024)S(1)} %pad_clamp_fusion), kind=kCustom, calls=%fused_computation.5 | custom fusion | bytes 50332416 | tf_op jit(solution)/shard_map/gather | solution.py:29
  321.0 15.3 %fusion.3 = f32[8,128,512,1]{2,1,3,0:T(8,128)} fusion(bf16[512,8,24,128]{3,0,2,1:T(8,128)(2,1)} %bitcast.139, bf16[2,8,24,128,128]{4,3,2,1,0:T(8,128)(2,1)} %param.13, pred[8,24]{1,0:T(8,128)(4,1)S(1)} %get-tuple-element.31), kind=kOutput, calls=%fused_computation.13 | convolution fusion | flops 3224371200 | bytes 33554624 | tf_op jit(solution)/shard_map/rtsk,tsck->rtc/dot_general | solution.py:32
  338.2 6.4 copy.31
  344.7 13.4 %gather_fusion.1 = bf16[192,512,128]{2,1,0:T(8,128)(2,1)} fusion(bf16[512,32,128]{2,0,1:T(8,128)(2,1)} %copy.31, s32[1024]{0:T(1024)S(1)} %pad_clamp_fusion.2), kind=kCustom, calls=%fused_computation.1 | custom fusion | bytes 50332416 | tf_op jit(solution)/shard_map/gather | solution.py:29
  358.0 15.2 %fusion.1 = f32[8,128,512,1]{2,1,3,0:T(8,128)} fusion(bf16[512,8,24,128]{3,0,2,1:T(8,128)(2,1)} %bitcast.137, bf16[2,8,24,128,128]{4,3,2,1,0:T(8,128)(2,1)} %param.13, pred[8,24]{1,0:T(8,128)(4,1)S(1)} %get-tuple-element.32), kind=kOutput, calls=%fused_computation.11 | convolution fusion | flops 3224371200 | bytes 33554624 | tf_op jit(solution)/shard_map/rtsk,tsck->rtc/dot_general | solution.py:32
  379.0 39.4 %all-reduce.1 = (f32[1]{0:T(128)}, f32[1]{0:T(128)}) all-reduce(f32[1]{0:T(128)} %bitcast.52, f32[1]{0:T(128)} %bitcast.18), channel_id=1, replica_groups=mesh['row'=8,'col'=4] {'row','col'}, use_global_device_ids=true, to_apply=%region_5.6 | all-reduce | flops 2 | bytes 16 | tf_op jit(solution)/shard_map/psum | solution.py:57
  427.1 125.0 %all-gather.27.cloned.1.call-done = bf16[8,512,1024]{2,1,0:T(8,128)(2,1)} async-done(((bf16[1,512,1024]{2,1,0:T(8,128)(2,1)}), bf16[8,512,1024]{2,1,0:T(8,128)(2,1)}) %all-gather.27.cloned.1.call-update) | async-done | bytes 8388624 | tf_op jit(solution)/shard_map/all_gather | solution.py:51
  552.2 14.1 %gather_fusion.6 = bf16[96,128,1024]{2,1,0:T(8,128)(2,1)} fusion(bf16[32,128,1024]{2,1,0:T(8,128)(2,1)} %bitcast.131, s32[1024]{0:T(1024)S(1)} %pad_clamp_fusion.1), kind=kCustom, calls=%fused_computation.6 | custom fusion | bytes 50332032 | tf_op jit(solution)/shard_map/gather | solution.py:15
  566.3 11.1 %bitcast_convert_fusion = bf16[4,128,1024]{2,1,0:T(8,128)(2,1)S(1)} fusion(bf16[4,24,128,1024]{3,2,1,0:T(8,128)(2,1)} %bitcast.132, bf16[2,4,24,128,128]{4,3,2,1,0:T(8,128)(2,1)} %param.10, pred[4,24]{1,0:T(4,128)(4,1)S(1)} %get-tuple-element.29), kind=kOutput, calls=%fused_computation.25 | convolution fusion | flops 3223322624 | bytes 29360224 | tf_op jit(solution)/shard_map/hgfu,hguq->hfq/dot_general | solution.py:18
  579.0 97.8 %all-gather.23.cloned.1.call-done = bf16[8,512,1024]{2,1,0:T(8,128)(2,1)} async-done(((bf16[1,512,1024]{2,1,0:T(8,128)(2,1)}), bf16[8,512,1024]{2,1,0:T(8,128)(2,1)}) %all-gather.23.cloned.1.call-update) | async-done | bytes 8388624 | tf_op jit(solution)/shard_map/all_gather | solution.py:51
  676.9 14.3 %gather_fusion.2 = bf16[96,128,1024]{2,1,0:T(8,128)(2,1)} fusion(bf16[32,128,1024]{2,1,0:T(8,128)(2,1)} %bitcast.130, s32[1024]{0:T(1024)S(1)} %pad_clamp_fusion.3), kind=kCustom, calls=%fused_computation.2 | custom fusion | bytes 50332032 | tf_op jit(solution)/shard_map/gather | solution.py:15
  691.1 11.1 %bitcast_convert_fusion.2 = bf16[4,128,1024]{2,1,0:T(8,128)(2,1)S(1)} fusion(bf16[4,24,128,1024]{3,2,1,0:T(8,128)(2,1)} %bitcast.133, bf16[2,4,24,128,128]{4,3,2,1,0:T(8,128)(2,1)} %param.10, pred[4,24]{1,0:T(4,128)(4,1)S(1)} %get-tuple-element.30), kind=kOutput, calls=%fused_computation.27 | convolution fusion | flops 3223322624 | bytes 29360224 | tf_op jit(solution)/shard_map/hgfu,hguq->hfq/dot_general | solution.py:18
  703.6 7.5 all-gather.19.cloned.1.call-done
  717.5 13.7 %gather_fusion.7 = bf16[192,512,128]{2,1,0:T(8,128)(2,1)} fusion(bf16[512,32,128]{2,0,1:T(8,128)(2,1)} %copy.40, s32[1024]{0:T(1024)S(1)} %pad_clamp_fusion), kind=kCustom, calls=%fused_computation.7 | custom fusion | bytes 50332416 | tf_op jit(solution)/shard_map/gather | solution.py:29
  731.2 15.3 %fusion.2 = f32[8,128,512,1]{2,1,3,0:T(8,128)} fusion(bf16[512,8,24,128]{3,0,2,1:T(8,128)(2,1)} %bitcast.134, bf16[2,8,24,128,128]{4,3,2,1,0:T(8,128)(2,1)} %param.13, pred[8,24]{1,0:T(8,128)(4,1)S(1)} %get-tuple-element.31), kind=kOutput, calls=%fused_computation.12 | convolution fusion | flops 3224371200 | bytes 33554624 | tf_op jit(solution)/shard_map/rtsk,tsck->rtc/dot_general | solution.py:32
  755.0 13.4 %gather_fusion.3 = bf16[192,512,128]{2,1,0:T(8,128)(2,1)} fusion(bf16[512,32,128]{2,0,1:T(8,128)(2,1)} %copy.34, s32[1024]{0:T(1024)S(1)} %pad_clamp_fusion.2), kind=kCustom, calls=%fused_computation.3 | custom fusion | bytes 50332416 | tf_op jit(solution)/shard_map/gather | solution.py:29
  768.3 15.2 %fusion = f32[8,128,512,1]{2,1,3,0:T(8,128)} fusion(bf16[512,8,24,128]{3,0,2,1:T(8,128)(2,1)} %bitcast.135, bf16[2,8,24,128,128]{4,3,2,1,0:T(8,128)(2,1)} %param.13, pred[8,24]{1,0:T(8,128)(4,1)S(1)} %get-tuple-element.32), kind=kOutput, calls=%fused_computation.10 | convolution fusion | flops 3224371200 | bytes 33554624 | tf_op jit(solution)/shard_map/rtsk,tsck->rtc/dot_general | solution.py:32
  789.3 39.4 %all-reduce = (f32[1]{0:T(128)}, f32[1]{0:T(128)}) all-reduce(f32[1]{0:T(128)} %bitcast.66, f32[1]{0:T(128)} %bitcast.32), channel_id=1, replica_groups=mesh['row'=8,'col'=4] {'row','col'}, use_global_device_ids=true, to_apply=%region_7.8 | all-reduce | flops 2 | bytes 16 | tf_op jit(solution)/shard_map/psum | solution.py:57
  (72 shorter events, 69.2 us)
Async XLA Ops:
  6.5 135.2 %all-gather.25.cloned.1.call-start = ((), (), s32[]{:S(2)}) async-start(), calls=%async_computation.6 | async-start | bytes 9437184 | tf_op jit(solution)/shard_map/all_gather | solution.py:51
  10.7 2.0 copy-start
  12.7 2.5 copy-start.2
  12.7 2.6 copy-start.3
  14.4 252.2 %all-gather.21.cloned.1.call-start = ((), (), s32[]{:S(2)}) async-start(), calls=%async_computation.4 | async-start | bytes 9437184 | tf_op jit(solution)/shard_map/all_gather | solution.py:51
  15.2 285.6 %all-gather.17.cloned.1.call-start = ((), (), s32[]{:S(2)}) async-start(), calls=%async_computation.2 | async-start | bytes 5242880 | tf_op jit(solution)/shard_map/all_gather | solution.py:54
  168.3 170.0 %all-gather.13.cloned.1.call-start = ((), (), s32[]{:S(2)}) async-start(), calls=%async_computation | async-start | bytes 5242880 | tf_op jit(solution)/shard_map/all_gather | solution.py:54
  280.8 12.8 %copy-start.1 = (s32[2,8,24]{2,1,0:T(8,128)S(1)}, s32[2,8,24]{2,1,0:T(8,128)}, u32[]{:S(2)}) copy-start(s32[2,8,24]{2,1,0:T(8,128)} %param.14) | copy-start | bytes 4612
  280.9 13.0 %copy-start.5 = (s32[2]{0:T(128)S(1)}, s32[2]{0:T(128)}, u32[]{:S(2)}) copy-start(s32[2]{0:T(128)} %param.17) | copy-start | bytes 28
  280.9 13.0 %copy-start.6 = (s32[2]{0:T(128)S(1)}, s32[2]{0:T(128)}, u32[]{:S(2)}) copy-start(s32[2]{0:T(128)} %param.16) | copy-start | bytes 28
  280.9 13.6 %copy-start.4 = (s32[2,8]{1,0:T(2,128)S(1)}, s32[2,8]{1,0:T(2,128)}, u32[]{:S(2)}) copy-start(s32[2,8]{1,0:T(2,128)} %param.15) | copy-start | bytes 196
  293.4 258.8 %all-gather.27.cloned.1.call-start = ((), (), s32[]{:S(2)}) async-start(), calls=%async_computation.7 | async-start | bytes 9437184 | tf_op jit(solution)/shard_map/all_gather | solution.py:51
  426.5 250.3 %all-gather.23.cloned.1.call-start = ((), (), s32[]{:S(2)}) async-start(), calls=%async_computation.5 | async-start | bytes 9437184 | tf_op jit(solution)/shard_map/all_gather | solution.py:51
  427.1 284.0 %all-gather.19.cloned.1.call-start = ((), (), s32[]{:S(2)}) async-start(), calls=%async_computation.3 | async-start | bytes 5242880 | tf_op jit(solution)/shard_map/all_gather | solution.py:54
  578.7 169.8 %all-gather.15.cloned.1.call-start = ((), (), s32[]{:S(2)}) async-start(), calls=%async_computation.1 | async-start | bytes 5242880 | tf_op jit(solution)/shard_map/all_gather | solution.py:54
Sparse Core Ops, SparseCore 0:
  14.5 127.1 all-gather.24
  143.9 122.6 all-gather.20
  268.1 32.6 all-gather.16
  302.2 34.4 all-gather.12
  426.6 125.5 all-gather.26
  554.2 122.6 all-gather.22
  678.4 32.6 all-gather.18
  712.6 34.4 all-gather.14
